TPU v7x, 8 devices: a whole 2x2x1 slice. The times are simulated.
8 devices in a mesh: rep: 2 (over z, y), nodes: 4 (over x, core).
Axes of the slice: x: 2, y: 2, z: 1, core: 2. Of those that a mesh axis runs over, the one named last changes fastest.
Arguments:
- adjacency: bfloat16 [8192, 8192], P('nodes')
- features: bfloat16 [8192, 128], P(('nodes', 'rep'))
- w_one: float32 [128, 128], replicated
- w_two: float32 [128, 40], replicated
- labels: int32 [8192], P(('nodes', 'rep'))
- label_mask: int32 [8192], P(('nodes', 'rep'))
Outputs:
- output 1: float32 [], replicated
- output 2: float32 [128, 128], replicated
- output 3: float32 [128, 40], replicated
All inputs are finite; a program needn't handle non-finite values.
Results may differ from a plain program's by a relative error of at most 0.001.
Values are sent between devices in bfloat16 or wider.
A program may use at most 1 GiB of HBM per device.

v0:
```python
import jax
import jax.numpy as jnp
from jax import lax
from jax.sharding import PartitionSpec as P


def solution(mesh):
    rep_size = mesh.shape["rep"]
    node_size = mesh.shape["nodes"]
    all_axes = ("rep", "nodes")

    def local_step(adj_rows, features, w_one, w_two, labels, label_mask):
        rows_dev = features.shape[0]
        group_rows_n = adj_rows.shape[0]
        num_classes = w_two.shape[1]
        adj_split = adj_rows.reshape(group_rows_n, node_size, rep_size, rows_dev)
        adj_mine = lax.dynamic_index_in_dim(adj_split, lax.axis_index("rep"), axis=2, keepdims=False)

        def aggregate(values):
            gathered = lax.all_gather(values, "nodes")
            partial_sum = jnp.einsum("ajb,jbf->af", adj_mine, gathered, preferred_element_type=jnp.float32)
            return lax.psum_scatter(partial_sum, "rep", scatter_dimension=0, tiled=True)

        def aggregate_t(grad_rows):
            group_grads = lax.all_gather(grad_rows, "rep", tiled=True)
            partial_sum = jnp.einsum("ajb,af->jbf", adj_mine, group_grads, preferred_element_type=jnp.float32)
            return lax.psum_scatter(partial_sum, "nodes", scatter_dimension=0, tiled=False)

        w_one_b = w_one.astype(jnp.bfloat16)
        w_two_b = w_two.astype(jnp.bfloat16)
        y_one = jnp.dot(features, w_one_b, preferred_element_type=jnp.float32).astype(jnp.bfloat16)
        z_one = aggregate(y_one)
        h_one = jnp.maximum(z_one, 0.0).astype(jnp.bfloat16)
        y_two = jnp.dot(h_one, w_two_b, preferred_element_type=jnp.float32).astype(jnp.bfloat16)
        z_two = aggregate(y_two)
        log_probs = jax.nn.log_softmax(z_two, axis=-1)
        onehot = (labels[:, None] == jnp.arange(num_classes)[None, :]).astype(jnp.float32)
        mask_f = label_mask.astype(jnp.float32)
        local_sums = jnp.stack([-jnp.sum(mask_f * jnp.sum(onehot * log_probs, axis=-1)), jnp.sum(mask_f)])
        global_sums = lax.psum(local_sums, all_axes)
        loss_value = global_sums[0] / global_sums[1]
        g_two = ((jnp.exp(log_probs) - onehot) * (mask_f / global_sums[1])[:, None]).astype(jnp.bfloat16)
        dy_two = aggregate_t(g_two).astype(jnp.bfloat16)
        dw_two = lax.psum(jnp.einsum("vh,vc->hc", h_one, dy_two, preferred_element_type=jnp.float32), all_axes)
        dh_one = jnp.einsum("vc,hc->vh", dy_two, w_two_b, preferred_element_type=jnp.float32)
        g_one = jnp.where(z_one > 0, dh_one, 0.0).astype(jnp.bfloat16)
        dy_one = aggregate_t(g_one).astype(jnp.bfloat16)
        dw_one = lax.psum(jnp.einsum("vf,vh->fh", features, dy_one, preferred_element_type=jnp.float32), all_axes)
        return loss_value, dw_one, dw_two

    row_spec = P(("nodes", "rep"))
    return jax.shard_map(local_step, mesh=mesh, in_specs=(P("nodes", None), P(("nodes", "rep"), None), P(), P(), row_spec, row_spec), out_specs=(P(), P(), P()), check_vma=False)
```

profile of v0, /device:TPU:0, one launch (start us, length us, event | category | flops | bytes accessed | tf_op | source)
XLA Modules:
  0.0 355.7 jit_solution(5374910349634718662)
XLA Ops:
  8.1 1.8 convolution_convert_fusion
  10.0 54.3 %reshape.18 = bf16[2048,4,2,1024]{3,2,1,0:T(2,128)(2,1)} reshape(bf16[2048,8192]{1,0:T(8,128)(2,1)} %param.6) | data formatting | bytes 67108864 | tf_op jit(solution)/shard_map/reshape | solution.py:16
  64.2 42.5 %constant_dynamic-slice_fusion = bf16[2048,4,1,1024]{3,2,1,0:T(2,128)(2,1)} fusion(bf16[2048,4,2,1024]{3,2,1,0:T(2,128)(2,1)} %reshape.18, s32[]{:T(128)S(6)} %select_n.8), kind=kLoop, calls=%fused_computation.33 | loop fusion | bytes 33554436 | tf_op jit(solution)/shard_map/jit(dynamic_index_in_dim)/dynamic_slice | solution.py:17
  106.8 22.0 %copy.25 = bf16[2048,4,1,1024]{3,0,1,2:T(8,128)(2,1)} copy(bf16[2048,4,1,1024]{3,2,1,0:T(2,128)(2,1)} %constant_dynamic-slice_fusion) | data formatting | bytes 33554432
  128.7 11.5 %convolution_bitcast_fusion = f32[2048,128]{1,0:T(8,128)} fusion(bf16[2048,4,1024]{2,0,1:T(8,128)(2,1)} %bitcast.40, bf16[4,1024,128]{2,1,0:T(8,128)(2,1)} %bitcast.45), kind=kOutput, calls=%fused_computation.1 | convolution fusion | flops 2147483648 | bytes 18874368 | tf_op jit(solution)/shard_map/ajb,jbf->af/dot_general | solution.py:21
  140.4 20.5 %reduce-scatter.9.cloned.1.call-done = f32[1024,128]{1,0:T(8,128)} async-done(((f32[2048,128]{1,0:T(8,128)}), f32[1024,128]{1,0:T(8,128)}) %reduce-scatter.9.cloned.1.call-update) | async-done | bytes 524304 | tf_op jit(solution)/shard_map/reduce_scatter | solution.py:22
  160.8 1.3 convolution_convert_fusion.1
  162.1 9.2 %all-gather.1 = bf16[4096,40]{0,1:T(8,128)(2,1)S(1)} all-gather(bf16[1024,40]{0,1:T(8,128)(2,1)S(1)} %convolution_convert_fusion.1), channel_id=3, replica_groups=mesh['rep'=2,'nodes'=4] {'nodes'}, dimensions={0}, use_global_device_ids=true | all-gather | bytes 409600 | tf_op jit(solution)/shard_map/all_gather | solution.py:20
  171.3 11.7 %convolution_bitcast_fusion.1 = f32[2048,40]{0,1:T(8,128)} fusion(bf16[2048,4,1024]{2,0,1:T(8,128)(2,1)} %bitcast.41, bf16[5,4,8,1024]{3,2,1,0:T(8,128)(2,1)S(1)} %bitcast.44), kind=kOutput, calls=%fused_computation.2 | convolution fusion | flops 671088640 | bytes 17432576 | tf_op jit(solution)/shard_map/ajb,jbf->af/dot_general | solution.py:21
  183.1 8.8 %reduce-scatter.11.cloned.1.call-done = f32[1024,40]{0,1:T(8,128)} async-done(((f32[2048,40]{0,1:T(8,128)}), f32[1024,40]{0,1:T(8,128)}) %reduce-scatter.11.cloned.1.call-update) | async-done | bytes 163856 | tf_op jit(solution)/shard_map/reduce_scatter | solution.py:22
  193.8 1.0 select_reduce_fusion
  196.7 22.4 %psum.21 = f32[2]{0:T(128)S(1)} all-reduce(f32[2]{0:T(128)S(1)} %pad_maximum_fusion), channel_id=1, replica_groups=mesh['rep'=2,'nodes'=4] {'rep','nodes'}, use_global_device_ids=true, to_apply=%region_7.8 | all-reduce | flops 2 | bytes 16 | tf_op jit(solution)/shard_map/psum | solution.py:40
  220.3 1.0 multiply_convert_fusion
  221.3 5.3 %all_gather.22 = bf16[2048,40]{0,1:T(8,128)(2,1)S(1)} all-gather(bf16[1024,40]{0,1:T(8,128)(2,1)S(1)} %multiply_convert_fusion), channel_id=1, replica_groups=mesh['rep'=2,'nodes'=4] {'rep'}, dimensions={0}, use_global_device_ids=true | all-gather | bytes 245760 | tf_op jit(solution)/shard_map/all_gather | solution.py:25
  226.7 10.5 %fusion.7 = f32[4,1024,40]{1,2,0:T(8,128)} fusion(bf16[2048,4,1024]{2,0,1:T(8,128)(2,1)} %bitcast.42, bf16[2048,40]{0,1:T(8,128)(2,1)S(1)} %all_gather.22), kind=kOutput, calls=%fused_computation.15 | convolution fusion | flops 671088640 | bytes 17596416 | tf_op jit(solution)/shard_map/ajb,af->jbf/dot_general | solution.py:26
  237.2 18.3 %reduce-scatter.13.cloned.1.call-done = f32[1,1024,40]{1,2,0:T(8,128)} async-done(((f32[4,1024,40]{1,2,0:T(8,128)}), f32[1,1024,40]{1,2,0:T(8,128)}) %reduce-scatter.13.cloned.1.call-update) | async-done | bytes 163856
  255.6 1.3 fusion
  256.8 8.5 %all_gather.23 = bf16[2048,128]{1,0:T(8,128)(2,1)S(1)} all-gather(bf16[1024,128]{1,0:T(8,128)(2,1)S(1)} %fusion), channel_id=1, replica_groups=mesh['rep'=2,'nodes'=4] {'rep'}, dimensions={0}, use_global_device_ids=true | all-gather | bytes 786432 | tf_op jit(solution)/shard_map/all_gather | solution.py:25
  265.3 9.7 %fusion.1 = f32[4,1024,128]{2,1,0:T(8,128)} fusion(bf16[2048,4,1024]{2,0,1:T(8,128)(2,1)} %bitcast.43, bf16[2048,128]{1,0:T(8,128)(2,1)S(1)} %all_gather.23), kind=kOutput, calls=%fused_computation.8 | convolution fusion | flops 2147483648 | bytes 19398656 | tf_op jit(solution)/shard_map/ajb,af->jbf/dot_general | solution.py:26
  276.4 24.3 %reduce-scatter.15.cloned.1.call-done = f32[1,1024,128]{2,1,0:T(8,128)} async-done(((f32[4,1024,128]{2,1,0:T(8,128)}), f32[1,1024,128]{2,1,0:T(8,128)}) %reduce-scatter.15.cloned.1.call-update) | async-done | bytes 524304
  300.7 1.9 convolution_bitcast_fusion.2
  302.9 22.7 %psum.23 = f32[128,40]{0,1:T(8,128)} all-reduce(f32[128,40]{0,1:T(8,128)S(1)} %fusion.9), channel_id=1, replica_groups=mesh['rep'=2,'nodes'=4] {'rep','nodes'}, use_global_device_ids=true, to_apply=%region_11.12 | all-reduce | flops 5120 | bytes 40960 | tf_op jit(solution)/shard_map/psum | solution.py:44
  325.6 20.6 %all-reduce.4.cloned.1.call-done = f32[128,128]{0,1:T(8,128)} async-done(((f32[128,128]{0,1:T(8,128)}), f32[128,128]{0,1:T(8,128)}) %all-reduce.4.cloned.1.call-update) | async-done | bytes 65552 | tf_op jit(solution)/shard_map/psum | solution.py:48
  346.1 1.6 copy.16
  (33 shorter events, 5.9 us)
Async XLA Ops:
  7.2 1.0 copy-start
  7.2 121.6 %all-gather.4.cloned.1.call-start = ((), (), s32[]{:S(2)}) async-start(), calls=%async_computation.7 | async-start | bytes 1310720 | tf_op jit(solution)/shard_map/all_gather | solution.py:20
  9.9 150.9 %reduce-scatter.9.cloned.1.call-start = ((), (), s32[]{:S(2)}) async-start(), calls=%async_computation.4 | async-start | bytes 1572864 | tf_op jit(solution)/shard_map/reduce_scatter | solution.py:22
  128.7 32.1 %copy-start.3 = (f32[128,40]{0,1:T(8,128)S(1)}, f32[128,40]{0,1:T(8,128)}, u32[]{:S(2)}) copy-start(f32[128,40]{0,1:T(8,128)} %param.9) | copy-start | bytes 61444
  140.3 53.5 %copy-start.4 = (s32[1024]{0:T(1024)S(1)}, s32[1024]{0:T(1024)}, u32[]{:S(2)}) copy-start(s32[1024]{0:T(1024)} %param.10) | copy-start | bytes 12292
  140.3 54.5 %copy-start.5 = (s32[1024]{0:T(1024)S(1)}, s32[1024]{0:T(1024)}, u32[]{:S(2)}) copy-start(s32[1024]{0:T(1024)} %param.11) | copy-start | bytes 12292
  140.3 51.6 %reduce-scatter.11.cloned.1.call-start = ((), (), s32[]{:S(2)}) async-start(), calls=%async_computation.5 | async-start | bytes 491520 | tf_op jit(solution)/shard_map/reduce_scatter | solution.py:22
  171.3 84.2 %copy-start.1 = (f32[1024,128]{1,0:T(8,128)S(1)}, f32[1024,128]{1,0:T(8,128)}, u32[]{:S(2)}) copy-start(f32[1024,128]{1,0:T(8,128)} %reduce-scatter.9.cloned.1.call-done) | copy-start | bytes 1572868
  183.0 72.5 %reduce-scatter.13.cloned.1.call-start = ((), (), s32[]{:S(2)}) async-start(), calls=%async_computation.8 | async-start | bytes 819200
  237.2 63.5 %reduce-scatter.15.cloned.1.call-start = ((), (), s32[]{:S(2)}) async-start(), calls=%async_computation.9 | async-start | bytes 2621440
  255.6 47.1 %copy-start.2 = (f32[1,1024,40]{1,2,0:T(8,128)S(1)}, f32[1,1024,40]{1,2,0:T(8,128)}, u32[]{:S(2)}) copy-start(f32[1,1024,40]{1,2,0:T(8,128)} %reduce-scatter.13.cloned.1.call-done) | copy-start | bytes 491524
  275.0 71.1 %all-reduce.4.cloned.1.call-start = ((), (), s32[]{:S(2)}) async-start(), calls=%async_computation.6 | async-start | bytes 131072 | tf_op jit(solution)/shard_map/psum | solution.py:48
Sparse Core Ops, SparseCore 0:
  10.0 16.5 all-gather.3
  140.4 20.3 reduce-scatter.8
  183.1 8.6 reduce-scatter.10
  237.3 18.2 reduce-scatter.12
  275.1 25.5 reduce-scatter.14
  304.2 41.9 all-reduce.3
where the time goes:
time: 358 us; the launch traced here: 356 us
  local copies, waits for them, and re-layouts  122 us (34%)
  waiting for transfers between devices  92.6 us (26%)
  blocking collectives  68.1 us (19%)
  matrix products  49.8 us (14%)
  between operations  17.3 us (5%)
  other arithmetic  5.8 us (2%)
    reshape x1, local copies, waits for them, and re-layouts, local_step(): adj_split = adj_rows.reshape(group_rows_n, node_size, rep_size, rows_dev)  54.3 us
    unnamed x8, waiting for transfers between devices  42.8 us
    dynamic_slice x1, local copies, waits for them, and re-layouts, local_step(): lax.dynamic_index_in_dim(adj_split, lax.axis_index('rep'), axis=2, keepdi...  42.5 us
    reduce_scatter x2, waiting for transfers between devices, aggregate(): return lax.psum_scatter(partial_sum, 'rep', scatter_dimension=0, tiled=True)  29.2 us
    unnamed x14, local copies, waits for them, and re-layouts  24.5 us
    dot_general x2, matrix products, aggregate(): jnp.einsum('ajb,jbf->af', adj_mine, gathered, preferred_element_type=jnp....  23.2 us
    psum x1, blocking collectives, local_step(): lax.psum(jnp.einsum('vh,vc->hc', h_one, dy_two, preferred_element_type=jn...  22.7 us
    psum x1, blocking collectives, local_step(): global_sums = lax.psum(local_sums, all_axes)  22.4 us
  transfers between devices with their start and end apart: 6, of which 5 were waited for; matrix products, arithmetic and copies ran while one was open for 33% of the time, Pallas kernels for 0%

commit v1 on v0

v1 whole, which is shorter than its diff:
```python
import jax
import jax.numpy as jnp
from jax import lax
from jax.experimental import pallas as pl
from jax.experimental.pallas import tpu as pltpu
from jax.sharding import PartitionSpec as P

MESH = pl.DeviceIdType.MESH
F32, BF16 = jnp.float32, jnp.bfloat16
NB = 1024
HALF = NB // 2
HID = 128
CLS = 40
PART = 176
PHALF = PART // 2
SAME_REP = (0, 1, 4, 5)


def dot(a, b, ca=1, cb=0):
    return lax.dot_general(a, b, (((ca,), (cb,)), ((), ())), preferred_element_type=F32)


def kernel(adj, feat, w1, w2, lab, msk, o_loss, o_dw1, o_dw2,
           a_own, a_oth, xg, acc, z1t, hl, h1, yg, gg, d2, d2r, cnt, part, pr, hs, tot,
           w1v, w2v, labv, mskv,
           a_sem, in_sem, xs, xr, ys, yr, gs, gr, ds_, dr, cs, cr, ps, pr_sem):
    r = lax.axis_index("rep")
    n = lax.axis_index("nodes")
    x, c = n // 2, n % 2

    def coords(rel):
        xx = 1 - x if rel & 4 else x
        yy = 1 - r if rel & 2 else r
        cc = 1 - c if rel & 1 else c
        return yy, 2 * xx + cc

    def peer(rel):
        yy, nn = coords(rel)
        return {"rep": yy, "nodes": nn}

    def column(rel):
        yy, nn = coords(rel)
        return pl.ds(pl.multiple_of((2 * nn + yy) * NB, NB), NB)

    def remote(src, dst, ssem, rsem, rel):
        return pltpu.make_async_remote_copy(src_ref=src, dst_ref=dst, send_sem=ssem, recv_sem=rsem,
                                            device_id=peer(rel), device_id_type=MESH)

    ins = [pltpu.make_async_copy(feat, xg.at[0], in_sem.at[0]),
           pltpu.make_async_copy(w1, w1v, in_sem.at[1]),
           pltpu.make_async_copy(w2, w2v, in_sem.at[2]),
           pltpu.make_async_copy(lab, labv, in_sem.at[3]),
           pltpu.make_async_copy(msk, mskv, in_sem.at[4])]
    for cp in ins:
        cp.start()
    own_rows = pl.ds(pl.multiple_of(r * NB, NB), NB)
    oth_rows = pl.ds(pl.multiple_of((1 - r) * NB, NB), NB)
    loads = {s: pltpu.make_async_copy(adj.at[own_rows, column(s)], a_own.at[s], a_sem.at[s]) for s in range(8)}
    oth_loads = [pltpu.make_async_copy(adj.at[oth_rows, column(s)], a_oth.at[k], a_sem.at[8 + k])
                 for k, s in enumerate(SAME_REP)]

    barrier = pltpu.get_barrier_semaphore()
    for s in range(1, 8):
        pl.semaphore_signal(barrier, inc=1, device_id=peer(s), device_id_type=MESH)
    for s in (0, 1, 4, 2, 5, 3, 6, 7):
        loads[s].start()
    for cp in oth_loads:
        cp.start()
    pl.semaphore_wait(barrier, 7)

    sent = []

    def go(cp):
        cp.start()
        sent.append(cp)
        return cp

    def gather(piece, ssem, rsem, use):
        def cp(k, src, dst, half, rel):
            return go(remote(piece(src, half), piece(dst, half), ssem.at[k], rsem.at[k], rel))
        x1 = cp(0, 0, 4, 1, 4)
        y0 = cp(1, 0, 2, 0, 2)
        p = cp(2, 0, 1, None, 1)
        x0 = cp(3, 0, 4, 0, 4)
        y1 = cp(4, 0, 2, 1, 2)
        use(0, None)
        p.wait_recv()
        use(1, None)
        x1.wait_recv()
        d61 = cp(5, 4, 6, 1, 2)
        d51 = cp(6, 4, 5, 1, 1)
        y0.wait_recv()
        d60 = cp(7, 2, 6, 0, 4)
        d30 = cp(8, 2, 3, 0, 1)
        use(4, 1)
        use(2, 0)
        x0.wait_recv()
        d50 = cp(9, 4, 5, 0, 1)
        y1.wait_recv()
        d31 = cp(10, 2, 3, 1, 1)
        use(4, 0)
        use(2, 1)
        d51.wait_recv()
        d50.wait_recv()
        use(5, None)
        d30.wait_recv()
        d31.wait_recv()
        use(3, None)
        d61.wait_recv()
        d71 = cp(11, 6, 7, 1, 1)
        d60.wait_recv()
        d70 = cp(12, 6, 7, 0, 1)
        use(6, None)
        d71.wait_recv()
        d70.wait_recv()
        use(7, None)

    for cp in ins:
        cp.wait()
    b1 = w1v[...].astype(BF16)
    b2t = w2v[...].astype(BF16)
    b2 = w2v[...].T.astype(BF16)
    mask = mskv[...].astype(F32)
    cnt[0] = jnp.broadcast_to(jnp.sum(mask, axis=1, keepdims=True), (8, 128))

    def xpiece(s, half):
        return xg.at[s] if half is None else xg.at[s, pl.ds(half * HALF, HALF), :]

    waited = set()

    def xuse(s, half):
        if s not in waited:
            loads[s].wait()
            waited.add(s)
        if half is None:
            xv, av = xg[s], a_own[s]
        else:
            xv, av = xg[s, half * HALF:(half + 1) * HALF, :], a_own[s, :, half * HALF:(half + 1) * HALF]
        rhs = jnp.concatenate([xv, dot(xv, b1).astype(BF16)], axis=1)
        prod = dot(av, rhs)
        if s == 0:
            acc[...] = prod
        else:
            acc[...] += prod

    gather(xpiece, xs, xr, xuse)
    counts = [go(remote(cnt.at[0], cnt.at[s], cs.at[s - 1], cr.at[s - 1], s)) for s in range(1, 8)]

    z1 = acc[:, HID:]
    h1[...] = jnp.maximum(z1, 0.0).astype(BF16)
    yg[0] = dot(b2t, h1[...], 1, 1).astype(BF16)

    z2 = []

    def ypiece(s, half):
        return yg.at[s] if half is None else yg.at[s, :, pl.ds(half * HALF, HALF)]

    def yuse(s, half):
        if half is None:
            yv, av = yg[s], a_own[s]
        else:
            yv, av = yg[s, :, half * HALF:(half + 1) * HALF], a_own[s, :, half * HALF:(half + 1) * HALF]
        prod = dot(yv, av, 1, 1)
        z2.append(prod if not z2 else z2.pop() + prod)
        if s == 0:
            z1t[...] = acc[:, HID:].T
            ax = acc[:, :HID]
            high = ax.astype(BF16)
            hl[:, :HID] = high
            hl[:, HID:] = (ax - high.astype(F32)).astype(BF16)

    gather(ypiece, ys, yr, yuse)
    z = z2[0]

    for cp in counts:
        cp.wait_recv()
    total = cnt[0][0:1, 0:1]
    for s in range(1, 8):
        total = total + cnt[s][0:1, 0:1]
    z = z - jnp.max(z, axis=0, keepdims=True)
    logp = z - jnp.log(jnp.sum(jnp.exp(z), axis=0, keepdims=True))
    onehot = (labv[...] == lax.broadcasted_iota(jnp.int32, (CLS, NB), 0)).astype(F32)
    loss = -jnp.sum(mask * jnp.sum(onehot * logp, axis=0, keepdims=True), axis=1, keepdims=True)
    gg[0] = ((jnp.exp(logp) - onehot) * (mask / total)).astype(BF16)
    g_y = go(remote(gg.at[0], gg.at[1], gs, gr, 2))

    for cp in oth_loads:
        cp.wait()
    g_own = gg[0]
    for k, s in ((3, 5), (2, 4), (1, 1), (0, 0)):
        d2[k] = dot(g_own, a_own[s])
    g_y.wait_recv()
    g_oth = gg[1]
    d2[3] += dot(g_oth, a_oth[3])
    pair_x = go(remote(d2.at[3], d2r.at[0], ds_.at[0], dr.at[0], 1))
    d2[2] += dot(g_oth, a_oth[2])
    d2[1] += dot(g_oth, a_oth[1])
    pair_o = go(remote(d2.at[1], d2r.at[1], ds_.at[1], dr.at[1], 1))
    pair_x.wait_recv()
    d2[2] += d2r[0]
    cross = go(remote(d2.at[2], d2r.at[2], ds_.at[2], dr.at[2], 4))
    d2[0] += dot(g_oth, a_oth[0])
    pair_o.wait_recv()
    chip_sum = d2[0] + d2r[1]
    cross.wait_recv()
    d2b = (chip_sum + d2r[2]).astype(BF16)

    g1 = jnp.where(z1t[...] > 0, dot(b2, d2b), 0.0).astype(BF16)
    dw1 = dot(g1, hl[...])
    part[0:HID] = dw1[:, :HID] + dw1[:, HID:]
    part[HID:HID + CLS] = dot(d2b, h1[...])
    part[HID + CLS:] = jnp.broadcast_to(loss, (8, 128))

    mine = pl.ds(pl.multiple_of(c * PHALF, 8), PHALF)
    theirs = pl.ds(pl.multiple_of((1 - c) * PHALF, 8), PHALF)
    a1 = go(remote(part.at[theirs, :], pr, ps.at[0], pr_sem.at[0], 1))
    a1.wait_recv()
    hs[0] = part[mine, :] + pr[...]
    a2 = [go(remote(hs.at[0], hs.at[k], ps.at[k], pr_sem.at[k], rel)) for k, rel in ((3, 6), (1, 4), (2, 2))]
    for cp in a2:
        cp.wait_recv()
    tot[mine, :] = (hs[0] + hs[1]) + (hs[2] + hs[3])
    a3 = go(remote(tot.at[mine, :], tot.at[mine, :], ps.at[4], pr_sem.at[4], 1))
    a3.wait_recv()
    o_dw1[...] = tot[0:HID].T
    o_dw2[...] = tot[HID:HID + CLS]
    o_loss[...] = tot[HID + CLS:HID + CLS + 1, 0:1] / total
    for cp in sent:
        cp.wait_send()


def solution(mesh):
    any_spec = pl.BlockSpec(memory_space=pl.ANY)
    vmem_spec = pl.BlockSpec(memory_space=pltpu.VMEM)
    dma = pltpu.SemaphoreType.DMA

    call = pl.pallas_call(
        kernel,
        out_shape=(jax.ShapeDtypeStruct((1, 1), F32), jax.ShapeDtypeStruct((HID, HID), F32),
                   jax.ShapeDtypeStruct((CLS, HID), F32)),
        in_specs=[any_spec] * 6,
        out_specs=(vmem_spec,) * 3,
        scratch_shapes=[
            pltpu.VMEM((8, NB, NB), BF16),
            pltpu.VMEM((4, NB, NB), BF16),
            pltpu.VMEM((8, NB, HID), BF16),
            pltpu.VMEM((NB, 2 * HID), F32),
            pltpu.VMEM((HID, NB), F32),
            pltpu.VMEM((NB, 2 * HID), BF16),
            pltpu.VMEM((NB, HID), BF16),
            pltpu.VMEM((8, CLS, NB), BF16),
            pltpu.VMEM((2, CLS, NB), BF16),
            pltpu.VMEM((4, CLS, NB), F32),
            pltpu.VMEM((3, CLS, NB), F32),
            pltpu.VMEM((8, 8, 128), F32),
            pltpu.VMEM((PART, 128), F32),
            pltpu.VMEM((PHALF, 128), F32),
            pltpu.VMEM((4, PHALF, 128), F32),
            pltpu.VMEM((PART, 128), F32),
            pltpu.VMEM((HID, HID), F32),
            pltpu.VMEM((CLS, HID), F32),
            pltpu.VMEM((1, NB), jnp.int32),
            pltpu.VMEM((1, NB), jnp.int32),
            dma((12,)), dma((5,)), dma((13,)), dma((13,)), dma((13,)), dma((13,)),
            dma, dma, dma((3,)), dma((3,)), dma((7,)), dma((7,)), dma((5,)), dma((5,)),
        ],
        compiler_params=pltpu.CompilerParams(collective_id=0, has_side_effects=True,
                                             vmem_limit_bytes=60 * 1024 * 1024),
        name="gcn_step",
    )

    def local_step(adj_rows, features, w_one, w_two, labels, label_mask):
        loss, dw1, dw2 = call(adj_rows, features, w_one, w_two.T, labels.reshape(1, NB), label_mask.reshape(1, NB))
        return loss.reshape(()), dw1, dw2.T

    row_spec = P(("nodes", "rep"))
    return jax.shard_map(local_step, mesh=mesh,
                         in_specs=(P("nodes", None), P(("nodes", "rep"), None), P(), P(), row_spec, row_spec),
                         out_specs=(P(), P(), P()), check_vma=False)
```

time: 358 us -> 53.9 us (0.15)
  local copies, waits for them, and re-layouts: 122 us -> 2.81 us
  waiting for transfers between devices: 92.6 us -> 0 us
  blocking collectives: 68.1 us -> 0 us
  matrix products: 49.8 us -> 0 us
  Pallas kernels: 0 us -> 48.4 us
  between operations: 17.3 us -> 2.46 us
  other arithmetic: 5.8 us -> 0 us
    reshape x1 -> x0, local copies, waits for them, and re-layouts: 54.3 us -> none  [local_step(): adj_split = adj_rows.reshape(group_rows_n, node_size, rep_size, rows_dev)]
    dot_general x9 -> x0, matrix products: 49.8 us -> none  [the longest x2 23.2 us: aggregate(): jnp.einsum('ajb,jbf->af', adj_mine, gathered, preferred_element_type=jnp....]
    pallas_call x0 -> x1, Pallas kernels: none -> 48.4 us  [local_step(): call(adj_rows, features, w_one, w_two.T, labels.reshape(1, NB), label_mas...]
    psum x2 -> x0, blocking collectives: 45.1 us -> none  [the longest x1 22.7 us: local_step(): lax.psum(jnp.einsum('vh,vc->hc', h_one, dy_two, preferred_element_type=jn...]
    unnamed x8 -> x0, waiting for transfers between devices: 42.8 us -> none
    dynamic_slice x1 -> x0, local copies, waits for them, and re-layouts: 42.5 us -> none  [local_step(): lax.dynamic_index_in_dim(adj_split, lax.axis_index('rep'), axis=2, keepdi...]
    reduce_scatter x2 -> x0, waiting for transfers between devices: 29.2 us -> none  [aggregate(): return lax.psum_scatter(partial_sum, 'rep', scatter_dimension=0, tiled=True)]
    all_gather x3 -> x0, blocking collectives: 23 us -> none  [the longest x2 13.8 us: aggregate_t(): group_grads = lax.all_gather(grad_rows, 'rep', tiled=True)]
  transfers between devices with their start and end apart: 6 -> 0, of which waited for: 5 -> 0; matrix products, arithmetic and copies ran while one was open for 33% -> 0% of each run, Pallas kernels for 0% -> 0%
where the time goes in v1:
time: 53.9 us; the launch traced here: 53.6 us
  Pallas kernels  48.4 us (90%)
  local copies, waits for them, and re-layouts  2.81 us (5%)
  between operations  2.46 us (5%)
    pallas_call x1, Pallas kernels, local_step(): call(adj_rows, features, w_one, w_two.T, labels.reshape(1, NB), label_mas...  48.4 us
    unnamed x2, local copies, waits for them, and re-layouts  2.81 us

profile of v1, /device:TPU:0, one launch (start us, length us, event | category | flops | bytes accessed | tf_op | source)
XLA Modules:
  0.0 53.6 jit_solution(6156441981757762927)
XLA Ops:
  0.6 48.4 %gcn_step.1 = (f32[1,1]{1,0:T(1,128)}, f32[128,128]{1,0:T(8,128)}, f32[40,128]{1,0:T(8,128)}) custom-call(bf16[2048,8192]{1,0:T(8,128)(2,1)} %adj.1, bf16[1024,128]{1,0:T(8,128)(2,1)} %feat.1, f32[128,128]{1,0:T(8,128)} %w1.1, f32[40,128]{1,0:T(8,128)} %bitcast.5, s32[1,1024]{1,0:T(1,128)} %bitcast.7, s32[1,1024]{1,0:T(1,128)} %bitcast.8), custom_call_target="tpu_custom_call" | custom-call | tf_op jit(solution)/shard_map/gcn_step/pallas_call | solution.py:273
  49.7 1.5 %copy.13 = f32[128,128]{1,0:T(8,128)} copy(f32[128,128]{1,0:T(8,128)} %get-tuple-element.13) | data formatting | bytes 131072
  51.2 1.3 %copy.14 = f32[128,40]{0,1:T(8,128)} copy(f32[128,40]{0,1:T(8,128)} %bitcast.6) | data formatting | bytes 40960

commit v2 on v1

--- a/solution.py
+++ b/solution.py
@@ -20,8 +20,8 @@
     return lax.dot_general(a, b, (((ca,), (cb,)), ((), ())), preferred_element_type=F32)
 
 
-def kernel(adj, feat, w1, w2, lab, msk, o_loss, o_dw1, o_dw2,
-           a_own, a_oth, xg, acc, z1t, hl, h1, yg, gg, d2, d2r, cnt, part, pr, hs, tot,
+def kernel(adj, feat, w1, w2, lab, msk, out,
+           a_own, a_oth, xg, rhs, acc, z2t, z1t, hl, h1, yg, gg, d2, d2r, cnt, part, pr, hs, tot,
            w1v, w2v, labv, mskv,
            a_sem, in_sem, xs, xr, ys, yr, gs, gr, ds_, dr, cs, cr, ps, pr_sem):
     r = lax.axis_index("rep")
@@ -75,45 +75,64 @@
         sent.append(cp)
         return cp
 
-    def gather(piece, ssem, rsem, use):
-        def cp(k, src, dst, half, rel):
-            return go(remote(piece(src, half), piece(dst, half), ssem.at[k], rsem.at[k], rel))
-        x1 = cp(0, 0, 4, 1, 4)
-        y0 = cp(1, 0, 2, 0, 2)
-        p = cp(2, 0, 1, None, 1)
-        x0 = cp(3, 0, 4, 0, 4)
-        y1 = cp(4, 0, 2, 1, 2)
-        use(0, None)
+    def rows(ref, s, lo, hi):
+        return ref.at[s, pl.ds(lo, hi - lo), :]
+
+    def lanes(ref, s, lo, hi):
+        return ref.at[s, :, pl.ds(lo, hi - lo)]
+
+    def gather(view, ref, ssem, rsem, use, cuts, idle):
+        k = iter(range(32))
+
+        def cp(src, dst, lo, hi, rel):
+            i = next(k)
+            return go(remote(view(ref, src, lo, hi), view(ref, dst, lo, hi), ssem.at[i], rsem.at[i], rel))
+
+        lo_half, hi_half = (0, HALF), (HALF, NB)
+        fine = HALF // cuts
+        x1 = cp(0, 4, *hi_half, 4)
+        y0 = cp(0, 2, *lo_half, 2)
+        p = cp(0, 1, 0, NB, 1)
+        x0 = cp(0, 4, *lo_half, 4)
+        y1 = cp(0, 2, *hi_half, 2)
+        use([(0, 0, NB)])
         p.wait_recv()
-        use(1, None)
+        use([(1, 0, NB)])
+        idle()
         x1.wait_recv()
-        d61 = cp(5, 4, 6, 1, 2)
-        d51 = cp(6, 4, 5, 1, 1)
+        d61 = [cp(4, 6, HALF + j * fine, HALF + (j + 1) * fine, 2) for j in range(cuts)]
+        d51 = cp(4, 5, *hi_half, 1)
         y0.wait_recv()
-        d60 = cp(7, 2, 6, 0, 4)
-        d30 = cp(8, 2, 3, 0, 1)
-        use(4, 1)
-        use(2, 0)
+        d60 = [cp(2, 6, j * fine, (j + 1) * fine, 4) for j in range(cuts)]
+        d30 = cp(2, 3, *lo_half, 1)
+        use([(4, *hi_half), (2, *lo_half)])
         x0.wait_recv()
-        d50 = cp(9, 4, 5, 0, 1)
+        d50 = cp(4, 5, *lo_half, 1)
         y1.wait_recv()
-        d31 = cp(10, 2, 3, 1, 1)
-        use(4, 0)
-        use(2, 1)
+        d31 = cp(2, 3, *hi_half, 1)
         d51.wait_recv()
+        d30.wait_recv()
+        use([(4, *lo_half), (2, *hi_half), (5, *hi_half), (3, *lo_half)])
         d50.wait_recv()
-        use(5, None)
-        d30.wait_recv()
         d31.wait_recv()
-        use(3, None)
-        d61.wait_recv()
-        d71 = cp(11, 6, 7, 1, 1)
-        d60.wait_recv()
-        d70 = cp(12, 6, 7, 0, 1)
-        use(6, None)
-        d71.wait_recv()
-        d70.wait_recv()
-        use(7, None)
+        use([(5, *lo_half), (3, *hi_half)])
+        late = []
+        for j in range(cuts):
+            lo, mid = j * fine, HALF + j * fine
+            d61[j].wait_recv()
+            d71 = cp(6, 7, mid, mid + fine, 1)
+            d60[j].wait_recv()
+            d70 = cp(6, 7, lo, lo + fine, 1)
+            here = [(6, mid, mid + fine), (6, lo, lo + fine)]
+            if late:
+                late[0].wait_recv()
+                late[1].wait_recv()
+                here += late[2]
+            use(here)
+            late = [d71, d70, [(7, mid, mid + fine), (7, lo, lo + fine)]]
+        late[0].wait_recv()
+        late[1].wait_recv()
+        use(late[2])
 
     for cp in ins:
         cp.wait()
@@ -123,54 +142,50 @@
     mask = mskv[...].astype(F32)
     cnt[0] = jnp.broadcast_to(jnp.sum(mask, axis=1, keepdims=True), (8, 128))
 
-    def xpiece(s, half):
-        return xg.at[s] if half is None else xg.at[s, pl.ds(half * HALF, HALF), :]
-
     waited = set()
 
-    def xuse(s, half):
-        if s not in waited:
-            loads[s].wait()
+    def xuse(pieces):
+        first = not waited
+        for s, lo, hi in pieces:
+            if s not in waited:
+                loads[s].wait()
             waited.add(s)
-        if half is None:
-            xv, av = xg[s], a_own[s]
-        else:
-            xv, av = xg[s, half * HALF:(half + 1) * HALF, :], a_own[s, :, half * HALF:(half + 1) * HALF]
-        rhs = jnp.concatenate([xv, dot(xv, b1).astype(BF16)], axis=1)
-        prod = dot(av, rhs)
-        if s == 0:
-            acc[...] = prod
-        else:
-            acc[...] += prod
-
-    gather(xpiece, xs, xr, xuse)
+            rhs[s, lo:hi, HID:] = dot(xg[s, lo:hi, :], b1).astype(BF16)
+            rhs[s, lo:hi, :HID] = xg[s, lo:hi, :]
+        for m in range(0, NB, 256):
+            prod = sum(dot(a_own[s, m:m + 256, lo:hi], rhs[s, lo:hi, :]) for s, lo, hi in pieces)
+            if not first:
+                acc[m:m + 256, :] += prod
+            else:
+                acc[m:m + 256, :] = prod
+
+    gather(rows, xg, xs, xr, xuse, 2, lambda: None)
     counts = [go(remote(cnt.at[0], cnt.at[s], cs.at[s - 1], cr.at[s - 1], s)) for s in range(1, 8)]
 
     z1 = acc[:, HID:]
     h1[...] = jnp.maximum(z1, 0.0).astype(BF16)
     yg[0] = dot(b2t, h1[...], 1, 1).astype(BF16)
 
-    z2 = []
-
-    def ypiece(s, half):
-        return yg.at[s] if half is None else yg.at[s, :, pl.ds(half * HALF, HALF)]
-
-    def yuse(s, half):
-        if half is None:
-            yv, av = yg[s], a_own[s]
-        else:
-            yv, av = yg[s, :, half * HALF:(half + 1) * HALF], a_own[s, :, half * HALF:(half + 1) * HALF]
-        prod = dot(yv, av, 1, 1)
-        z2.append(prod if not z2 else z2.pop() + prod)
-        if s == 0:
-            z1t[...] = acc[:, HID:].T
-            ax = acc[:, :HID]
-            high = ax.astype(BF16)
-            hl[:, :HID] = high
-            hl[:, HID:] = (ax - high.astype(F32)).astype(BF16)
-
-    gather(ypiece, ys, yr, yuse)
-    z = z2[0]
+    started = []
+
+    def yuse(pieces):
+        for m in range(0, NB, HALF):
+            prod = sum(dot(yg[s, :, lo:hi], a_own[s, m:m + HALF, lo:hi], 1, 1) for s, lo, hi in pieces)
+            if started:
+                z2t[:, m:m + HALF] += prod
+            else:
+                z2t[:, m:m + HALF] = prod
+        started.append(1)
+
+    def keep_for_backward():
+        z1t[...] = acc[:, HID:].T
+        ax = acc[:, :HID]
+        high = ax.astype(BF16)
+        hl[:, :HID] = high
+        hl[:, HID:] = (ax - high.astype(F32)).astype(BF16)
+
+    gather(lanes, yg, ys, yr, yuse, 1, keep_for_backward)
+    z = z2t[...]
 
     for cp in counts:
         cp.wait_recv()
@@ -191,19 +206,25 @@
         d2[k] = dot(g_own, a_own[s])
     g_y.wait_recv()
     g_oth = gg[1]
-    d2[3] += dot(g_oth, a_oth[3])
-    pair_x = go(remote(d2.at[3], d2r.at[0], ds_.at[0], dr.at[0], 1))
+    halves = ((0, HALF), (HALF, NB))
+    pair_x = []
+    for j, (lo, hi) in enumerate(halves):
+        d2[3, :, lo:hi] += dot(g_oth, a_oth[3, :, lo:hi])
+        pair_x.append(go(remote(lanes(d2, 3, lo, hi), lanes(d2r, 0, lo, hi), ds_.at[j], dr.at[j], 1)))
     d2[2] += dot(g_oth, a_oth[2])
+    cross = []
+    for j, (lo, hi) in enumerate(halves):
+        pair_x[j].wait_recv()
+        d2[2, :, lo:hi] += d2r[0, :, lo:hi]
+        cross.append(go(remote(lanes(d2, 2, lo, hi), lanes(d2r, 2, lo, hi), ds_.at[2 + j], dr.at[2 + j], 4)))
     d2[1] += dot(g_oth, a_oth[1])
-    pair_o = go(remote(d2.at[1], d2r.at[1], ds_.at[1], dr.at[1], 1))
-    pair_x.wait_recv()
-    d2[2] += d2r[0]
-    cross = go(remote(d2.at[2], d2r.at[2], ds_.at[2], dr.at[2], 4))
+    pair_o = go(remote(d2.at[1], d2r.at[1], ds_.at[4], dr.at[4], 1))
     d2[0] += dot(g_oth, a_oth[0])
     pair_o.wait_recv()
-    chip_sum = d2[0] + d2r[1]
-    cross.wait_recv()
-    d2b = (chip_sum + d2r[2]).astype(BF16)
+    d2[0] += d2r[1]
+    cross[0].wait_recv()
+    cross[1].wait_recv()
+    d2b = (d2[0] + d2r[2]).astype(BF16)
 
     g1 = jnp.where(z1t[...] > 0, dot(b2, d2b), 0.0).astype(BF16)
     dw1 = dot(g1, hl[...])
@@ -222,11 +243,16 @@
     tot[mine, :] = (hs[0] + hs[1]) + (hs[2] + hs[3])
     a3 = go(remote(tot.at[mine, :], tot.at[mine, :], ps.at[4], pr_sem.at[4], 1))
     a3.wait_recv()
-    o_dw1[...] = tot[0:HID].T
-    o_dw2[...] = tot[HID:HID + CLS]
-    o_loss[...] = tot[HID + CLS:HID + CLS + 1, 0:1] / total
+    out[0:HID + CLS, :] = tot[0:HID + CLS, :]
+    out[HID + CLS:, :] = tot[HID + CLS:, :] / total
     for cp in sent:
         cp.wait_send()
+
+
+def unpack(packed, o_loss, o_dw1, o_dw2):
+    o_dw1[...] = packed[0:HID].T
+    o_dw2[...] = packed[HID:HID + CLS]
+    o_loss[...] = packed[HID + CLS:HID + CLS + 1, 0:1]
 
 
 def solution(mesh):
@@ -236,15 +262,16 @@
 
     call = pl.pallas_call(
         kernel,
-        out_shape=(jax.ShapeDtypeStruct((1, 1), F32), jax.ShapeDtypeStruct((HID, HID), F32),
-                   jax.ShapeDtypeStruct((CLS, HID), F32)),
+        out_shape=jax.ShapeDtypeStruct((PART, 128), F32),
         in_specs=[any_spec] * 6,
-        out_specs=(vmem_spec,) * 3,
+        out_specs=vmem_spec,
         scratch_shapes=[
             pltpu.VMEM((8, NB, NB), BF16),
             pltpu.VMEM((4, NB, NB), BF16),
             pltpu.VMEM((8, NB, HID), BF16),
+            pltpu.VMEM((8, NB, 2 * HID), BF16),
             pltpu.VMEM((NB, 2 * HID), F32),
+            pltpu.VMEM((CLS, NB), F32),
             pltpu.VMEM((HID, NB), F32),
             pltpu.VMEM((NB, 2 * HID), BF16),
             pltpu.VMEM((NB, HID), BF16),
@@ -261,16 +288,26 @@
             pltpu.VMEM((CLS, HID), F32),
             pltpu.VMEM((1, NB), jnp.int32),
             pltpu.VMEM((1, NB), jnp.int32),
-            dma((12,)), dma((5,)), dma((13,)), dma((13,)), dma((13,)), dma((13,)),
-            dma, dma, dma((3,)), dma((3,)), dma((7,)), dma((7,)), dma((5,)), dma((5,)),
+            dma((12,)), dma((5,)), dma((17,)), dma((17,)), dma((13,)), dma((13,)),
+            dma, dma, dma((5,)), dma((5,)), dma((7,)), dma((7,)), dma((5,)), dma((5,)),
         ],
         compiler_params=pltpu.CompilerParams(collective_id=0, has_side_effects=True,
                                              vmem_limit_bytes=60 * 1024 * 1024),
         name="gcn_step",
     )
 
+    unpack_call = pl.pallas_call(
+        unpack,
+        out_shape=(jax.ShapeDtypeStruct((1, 1), F32), jax.ShapeDtypeStruct((HID, HID), F32),
+                   jax.ShapeDtypeStruct((CLS, HID), F32)),
+        in_specs=[vmem_spec],
+        out_specs=(vmem_spec,) * 3,
+        name="unpack",
+    )
+
     def local_step(adj_rows, features, w_one, w_two, labels, label_mask):
-        loss, dw1, dw2 = call(adj_rows, features, w_one, w_two.T, labels.reshape(1, NB), label_mask.reshape(1, NB))
+        packed = call(adj_rows, features, w_one, w_two.T, labels.reshape(1, NB), label_mask.reshape(1, NB))
+        loss, dw1, dw2 = unpack_call(packed)
         return loss.reshape(()), dw1, dw2.T
 
     row_spec = P(("nodes", "rep"))

time: 53.9 us -> 46.7 us (0.87)
  local copies, waits for them, and re-layouts: 2.81 us -> 0 us
  Pallas kernels: 48.4 us -> 46 us
  between operations: 2.46 us -> 0.64 us
    pallas_call x1, Pallas kernels: 48.4 us -> 44.3 us  [local_step(): call(adj_rows, features, w_one, w_two.T, labels.reshape(1, NB), label_mas...]
    unnamed x2 -> x0, local copies, waits for them, and re-layouts: 2.81 us -> none
    pallas_call x0 -> x1, Pallas kernels: none -> 1.62 us  [local_step(): loss, dw1, dw2 = unpack_call(packed)]
where the time goes in v2:
time: 46.7 us; the launch traced here: 46.6 us
  Pallas kernels  46 us (99%)
  between operations  0.64 us (1%)
    pallas_call x1, Pallas kernels, local_step(): call(adj_rows, features, w_one, w_two.T, labels.reshape(1, NB), label_mas...  44.3 us
    pallas_call x1, Pallas kernels, local_step(): loss, dw1, dw2 = unpack_call(packed)  1.62 us

profile of v2, /device:TPU:0, one launch (start us, length us, event | category | flops | bytes accessed | tf_op | source)
XLA Modules:
  0.0 46.6 jit_solution(15436370115669234389)
XLA Ops:
  0.6 44.3 %gcn_step.1.packed = f32[176,128]{1,0:T(8,128)} custom-call(bf16[2048,8192]{1,0:T(8,128)(2,1)} %adj.1, bf16[1024,128]{1,0:T(8,128)(2,1)} %feat.1, f32[128,128]{1,0:T(8,128)} %w1.1, f32[40,128]{1,0:T(8,128)} %bitcast.5, s32[1,1024]{1,0:T(1,128)} %bitcast.6, s32[1,1024]{1,0:T(1,128)} %bitcast.7), custom_call_target="tpu_custom_call" | custom-call | tf_op jit(solution)/shard_map/gcn_step/pallas_call | solution.py:309
  45.0 1.6 %unpack.1 = (f32[1,1]{1,0:T(1,128)}, f32[128,128]{1,0:T(8,128)}, f32[40,128]{1,0:T(8,128)}) custom-call(f32[176,128]{1,0:T(8,128)} %gcn_step.1.packed), custom_call_target="tpu_custom_call" | custom-call | tf_op jit(solution)/shard_map/unpack/pallas_call | solution.py:310

commit v3 on v2

--- a/solution.py
+++ b/solution.py
@@ -9,6 +9,7 @@
 F32, BF16 = jnp.float32, jnp.bfloat16
 NB = 1024
 HALF = NB // 2
+XP = 256
 HID = 128
 CLS = 40
 PART = 176
@@ -60,13 +61,16 @@
                  for k, s in enumerate(SAME_REP)]
 
     barrier = pltpu.get_barrier_semaphore()
-    for s in range(1, 8):
+    for s in (1, 2, 4):
         pl.semaphore_signal(barrier, inc=1, device_id=peer(s), device_id_type=MESH)
     for s in (0, 1, 4, 2, 5, 3, 6, 7):
         loads[s].start()
     for cp in oth_loads:
         cp.start()
-    pl.semaphore_wait(barrier, 7)
+    pl.semaphore_wait(barrier, 3)
+
+    def lanes(ref, s, lo, hi):
+        return ref.at[s, :, pl.ds(lo, hi - lo)]
 
     sent = []
 
@@ -75,64 +79,53 @@
         sent.append(cp)
         return cp
 
-    def rows(ref, s, lo, hi):
-        return ref.at[s, pl.ds(lo, hi - lo), :]
-
-    def lanes(ref, s, lo, hi):
-        return ref.at[s, :, pl.ds(lo, hi - lo)]
-
-    def gather(view, ref, ssem, rsem, use, cuts, idle):
+    def gather(view, n, ssem, rsem, use, idle):
         k = iter(range(32))
 
-        def cp(src, dst, lo, hi, rel):
+        def cp(src, dst, piece, rel):
             i = next(k)
-            return go(remote(view(ref, src, lo, hi), view(ref, dst, lo, hi), ssem.at[i], rsem.at[i], rel))
-
-        lo_half, hi_half = (0, HALF), (HALF, NB)
-        fine = HALF // cuts
-        x1 = cp(0, 4, *hi_half, 4)
-        y0 = cp(0, 2, *lo_half, 2)
-        p = cp(0, 1, 0, NB, 1)
-        x0 = cp(0, 4, *lo_half, 4)
-        y1 = cp(0, 2, *hi_half, 2)
-        use([(0, 0, NB)])
+            return go(remote(view(src, piece), view(dst, piece), ssem.at[i], rsem.at[i], rel))
+
+        low, high = list(range(n // 2)), list(range(n // 2, n))
+        xseq, yseq = high + low, low + high
+        xs_, ys_ = [], []
+        for j in range(n):
+            xs_.append(cp(0, 4, xseq[j], 4))
+            ys_.append(cp(0, 2, yseq[j], 2))
+            if j == 0:
+                p = cp(0, 1, None, 1)
+        use([(0, i) for i in range(n)])
         p.wait_recv()
-        use([(1, 0, NB)])
+        use([(1, i) for i in range(n)])
         idle()
-        x1.wait_recv()
-        d61 = [cp(4, 6, HALF + j * fine, HALF + (j + 1) * fine, 2) for j in range(cuts)]
-        d51 = cp(4, 5, *hi_half, 1)
-        y0.wait_recv()
-        d60 = [cp(2, 6, j * fine, (j + 1) * fine, 4) for j in range(cuts)]
-        d30 = cp(2, 3, *lo_half, 1)
-        use([(4, *hi_half), (2, *lo_half)])
-        x0.wait_recv()
-        d50 = cp(4, 5, *lo_half, 1)
-        y1.wait_recv()
-        d31 = cp(2, 3, *hi_half, 1)
-        d51.wait_recv()
-        d30.wait_recv()
-        use([(4, *lo_half), (2, *hi_half), (5, *hi_half), (3, *lo_half)])
-        d50.wait_recv()
-        d31.wait_recv()
-        use([(5, *lo_half), (3, *hi_half)])
-        late = []
-        for j in range(cuts):
-            lo, mid = j * fine, HALF + j * fine
-            d61[j].wait_recv()
-            d71 = cp(6, 7, mid, mid + fine, 1)
-            d60[j].wait_recv()
-            d70 = cp(6, 7, lo, lo + fine, 1)
-            here = [(6, mid, mid + fine), (6, lo, lo + fine)]
-            if late:
-                late[0].wait_recv()
-                late[1].wait_recv()
-                here += late[2]
-            use(here)
-            late = [d71, d70, [(7, mid, mid + fine), (7, lo, lo + fine)]]
-        late[0].wait_recv()
-        late[1].wait_recv()
-        use(late[2])
+        held, via_y, via_x = None, [], []
+
+        def take_held():
+            held[0].wait_recv()
+            held[1].wait_recv()
+            return held[2]
+
+        for j in range(n):
+            xs_[j].wait_recv()
+            if j < n // 2:
+                via_y.append(cp(4, 6, xseq[j], 2))
+            f5 = cp(4, 5, xseq[j], 1)
+            ys_[j].wait_recv()
+            if j < n // 2:
+                via_x.append(cp(2, 6, yseq[j], 4))
+            f3 = cp(2, 3, yseq[j], 1)
+            use([(4, xseq[j]), (2, yseq[j])] + (take_held() if held else []))
+            held = (f5, f3, [(5, xseq[j]), (3, yseq[j])])
+        use(take_held())
+        held = None
+        for j in range(n // 2):
+            via_y[j].wait_recv()
+            f7y = cp(6, 7, xseq[j], 1)
+            via_x[j].wait_recv()
+            f7x = cp(6, 7, yseq[j], 1)
+            use([(6, xseq[j]), (6, yseq[j])] + (take_held() if held else []))
+            held = (f7y, f7x, [(7, xseq[j]), (7, yseq[j])])
+        use(take_held())
 
     for cp in ins:
         cp.wait()
@@ -144,33 +137,47 @@
 
     waited = set()
 
+    def xview(s, piece):
+        return xg.at[s] if piece is None else xg.at[s, pl.ds(piece * XP, XP), :]
+
     def xuse(pieces):
         first = not waited
-        for s, lo, hi in pieces:
+        parts = []
+        for s, i in pieces:
             if s not in waited:
                 loads[s].wait()
             waited.add(s)
+            if parts and parts[-1][0] == s and parts[-1][2] == i * XP:
+                parts[-1][2] += XP
+            else:
+                parts.append([s, i * XP, i * XP + XP])
+        for s, lo, hi in parts:
             rhs[s, lo:hi, HID:] = dot(xg[s, lo:hi, :], b1).astype(BF16)
             rhs[s, lo:hi, :HID] = xg[s, lo:hi, :]
         for m in range(0, NB, 256):
-            prod = sum(dot(a_own[s, m:m + 256, lo:hi], rhs[s, lo:hi, :]) for s, lo, hi in pieces)
-            if not first:
+            prod = sum(dot(a_own[s, m:m + 256, lo:hi], rhs[s, lo:hi, :]) for s, lo, hi in parts)
+            if first:
+                acc[m:m + 256, :] = prod
+            else:
                 acc[m:m + 256, :] += prod
-            else:
-                acc[m:m + 256, :] = prod
-
-    gather(rows, xg, xs, xr, xuse, 2, lambda: None)
+
+    gather(xview, NB // XP, xs, xr, xuse, lambda: None)
     counts = [go(remote(cnt.at[0], cnt.at[s], cs.at[s - 1], cr.at[s - 1], s)) for s in range(1, 8)]
 
     z1 = acc[:, HID:]
     h1[...] = jnp.maximum(z1, 0.0).astype(BF16)
-    yg[0] = dot(b2t, h1[...], 1, 1).astype(BF16)
+    y2 = dot(b2t, h1[...], 1, 1).astype(BF16)
+    yg[0, 0] = y2[:, :HALF]
+    yg[0, 1] = y2[:, HALF:]
 
     started = []
+
+    def yview(s, piece):
+        return yg.at[s] if piece is None else yg.at[s, piece]
 
     def yuse(pieces):
         for m in range(0, NB, HALF):
-            prod = sum(dot(yg[s, :, lo:hi], a_own[s, m:m + HALF, lo:hi], 1, 1) for s, lo, hi in pieces)
+            prod = sum(dot(yg[s, i], a_own[s, m:m + HALF, i * HALF:(i + 1) * HALF], 1, 1) for s, i in pieces)
             if started:
                 z2t[:, m:m + HALF] += prod
             else:
@@ -184,7 +191,7 @@
         hl[:, :HID] = high
         hl[:, HID:] = (ax - high.astype(F32)).astype(BF16)
 
-    gather(lanes, yg, ys, yr, yuse, 1, keep_for_backward)
+    gather(yview, 2, ys, yr, yuse, keep_for_backward)
     z = z2t[...]
 
     for cp in counts:
@@ -196,30 +203,35 @@
     logp = z - jnp.log(jnp.sum(jnp.exp(z), axis=0, keepdims=True))
     onehot = (labv[...] == lax.broadcasted_iota(jnp.int32, (CLS, NB), 0)).astype(F32)
     loss = -jnp.sum(mask * jnp.sum(onehot * logp, axis=0, keepdims=True), axis=1, keepdims=True)
-    gg[0] = ((jnp.exp(logp) - onehot) * (mask / total)).astype(BF16)
-    g_y = go(remote(gg.at[0], gg.at[1], gs, gr, 2))
+    g2 = ((jnp.exp(logp) - onehot) * (mask / total)).astype(BF16)
+    halves = ((0, HALF), (HALF, NB))
+    g_y = []
+    for j, (lo, hi) in enumerate(halves):
+        gg[0, j] = g2[:, lo:hi]
+        g_y.append(go(remote(gg.at[0, j], gg.at[1, j], gs.at[j], gr.at[j], 2)))
 
     for cp in oth_loads:
         cp.wait()
-    g_own = gg[0]
     for k, s in ((3, 5), (2, 4), (1, 1), (0, 0)):
-        d2[k] = dot(g_own, a_own[s])
-    g_y.wait_recv()
-    g_oth = gg[1]
-    halves = ((0, HALF), (HALF, NB))
+        d2[k] = sum(dot(gg[0, j], a_own[s, lo:hi, :]) for j, (lo, hi) in enumerate(halves))
+    g_y[0].wait_recv()
+    for k in (3, 2, 1, 0):
+        d2[k] += dot(gg[1, 0], a_oth[k, 0:HALF, :])
+    g_y[1].wait_recv()
+    g_oth = gg[1, 1]
     pair_x = []
     for j, (lo, hi) in enumerate(halves):
-        d2[3, :, lo:hi] += dot(g_oth, a_oth[3, :, lo:hi])
+        d2[3, :, lo:hi] += dot(g_oth, a_oth[3, HALF:, lo:hi])
         pair_x.append(go(remote(lanes(d2, 3, lo, hi), lanes(d2r, 0, lo, hi), ds_.at[j], dr.at[j], 1)))
-    d2[2] += dot(g_oth, a_oth[2])
+    d2[2] += dot(g_oth, a_oth[2, HALF:, :])
     cross = []
     for j, (lo, hi) in enumerate(halves):
         pair_x[j].wait_recv()
         d2[2, :, lo:hi] += d2r[0, :, lo:hi]
         cross.append(go(remote(lanes(d2, 2, lo, hi), lanes(d2r, 2, lo, hi), ds_.at[2 + j], dr.at[2 + j], 4)))
-    d2[1] += dot(g_oth, a_oth[1])
+    d2[1] += dot(g_oth, a_oth[1, HALF:, :])
     pair_o = go(remote(d2.at[1], d2r.at[1], ds_.at[4], dr.at[4], 1))
-    d2[0] += dot(g_oth, a_oth[0])
+    d2[0] += dot(g_oth, a_oth[0, HALF:, :])
     pair_o.wait_recv()
     d2[0] += d2r[1]
     cross[0].wait_recv()
@@ -275,8 +287,8 @@
             pltpu.VMEM((HID, NB), F32),
             pltpu.VMEM((NB, 2 * HID), BF16),
             pltpu.VMEM((NB, HID), BF16),
-            pltpu.VMEM((8, CLS, NB), BF16),
-            pltpu.VMEM((2, CLS, NB), BF16),
+            pltpu.VMEM((8, 2, CLS, HALF), BF16),
+            pltpu.VMEM((2, 2, CLS, HALF), BF16),
             pltpu.VMEM((4, CLS, NB), F32),
             pltpu.VMEM((3, CLS, NB), F32),
             pltpu.VMEM((8, 8, 128), F32),
@@ -288,11 +300,11 @@
             pltpu.VMEM((CLS, HID), F32),
             pltpu.VMEM((1, NB), jnp.int32),
             pltpu.VMEM((1, NB), jnp.int32),
-            dma((12,)), dma((5,)), dma((17,)), dma((17,)), dma((13,)), dma((13,)),
-            dma, dma, dma((5,)), dma((5,)), dma((7,)), dma((7,)), dma((5,)), dma((5,)),
+            dma((12,)), dma((5,)), dma((25,)), dma((25,)), dma((13,)), dma((13,)),
+            dma((2,)), dma((2,)), dma((5,)), dma((5,)), dma((7,)), dma((7,)), dma((5,)), dma((5,)),
         ],
         compiler_params=pltpu.CompilerParams(collective_id=0, has_side_effects=True,
-                                             vmem_limit_bytes=60 * 1024 * 1024),
+                                             vmem_limit_bytes=40 << 20),
         name="gcn_step",
     )
 
@@ -302,11 +314,13 @@
                    jax.ShapeDtypeStruct((CLS, HID), F32)),
         in_specs=[vmem_spec],
         out_specs=(vmem_spec,) * 3,
+        compiler_params=pltpu.CompilerParams(vmem_limit_bytes=4 << 20),
         name="unpack",
     )
 
     def local_step(adj_rows, features, w_one, w_two, labels, label_mask):
-        packed = call(adj_rows, features, w_one, w_two.T, labels.reshape(1, NB), label_mask.reshape(1, NB))
+        operands = (adj_rows, features, w_one, w_two.T, labels.reshape(1, NB), label_mask.reshape(1, NB))
+        packed = call(*(pltpu.with_memory_space_constraint(v, pltpu.HBM) for v in operands))
         loss, dw1, dw2 = unpack_call(packed)
         return loss.reshape(()), dw1, dw2.T
 

time: 46.7 us -> 44.3 us (0.949)
  Pallas kernels: 46 us -> 43.6 us
    pallas_call x1, Pallas kernels: 44.3 us -> 42.9 us  [local_step(): call(*(pltpu.with_memory_space_constraint(v, pltpu.HBM) for v in operands))]
    pallas_call x1, Pallas kernels: 1.62 us -> 0.73 us  [local_step(): loss, dw1, dw2 = unpack_call(packed)]
where the time goes in v3:
time: 44.3 us; the launch traced here: 44.2 us
  Pallas kernels  43.6 us (98%)
  between operations  0.64 us (1%)
    pallas_call x1, Pallas kernels, local_step(): call(*(pltpu.with_memory_space_constraint(v, pltpu.HBM) for v in operands))  42.9 us

profile of v3, /device:TPU:0, one launch (start us, length us, event | category | flops | bytes accessed | tf_op | source)
XLA Modules:
  0.0 44.2 jit_solution(1548389138763874245)
XLA Ops:
  0.6 42.9 %gcn_step.1.packed = f32[176,128]{1,0:T(8,128)S(1)} custom-call(bf16[2048,8192]{1,0:T(8,128)(2,1)} %adj.1, bf16[1024,128]{1,0:T(8,128)(2,1)} %feat.1, f32[128,128]{1,0:T(8,128)} %w1.1, f32[40,128]{1,0:T(8,128)} %bitcast.5, s32[1,1024]{1,0:T(1,128)} %bitcast.6, s32[1,1024]{1,0:T(1,128)} %bitcast.7), custom_call_target="tpu_custom_call" | custom-call | tf_op jit(solution)/shard_map/gcn_step/pallas_call | solution.py:323
  43.5 0.7 %unpack.1 = (f32[1,1]{1,0:T(1,128)}, f32[128,128]{1,0:T(8,128)}, f32[40,128]{1,0:T(8,128)}) custom-call(f32[176,128]{1,0:T(8,128)S(1)} %gcn_step.1.packed), custom_call_target="tpu_custom_call" | custom-call | tf_op jit(solution)/shard_map/unpack/pallas_call | solution.py:324

commit v4 on v3

v4 whole, which is shorter than its diff:
```python
import jax
import jax.numpy as jnp
from jax import lax
from jax.experimental import pallas as pl
from jax.experimental.pallas import tpu as pltpu
from jax.sharding import PartitionSpec as P

MESH = pl.DeviceIdType.MESH
F32, BF16 = jnp.float32, jnp.bfloat16
NB = 1024
HALF = NB // 2
PIECES = 4
XP = NB // PIECES
HID = 128
CLS = 40
PART = 176
PHALF = PART // 2


def dot(a, b, ca=1, cb=0):
    return lax.dot_general(a, b, (((ca,), (cb,)), ((), ())), preferred_element_type=F32)


def kernel(adj, feat, w1, w2, lab, msk, out,
           a_own, xg, rhs, acc, z2t, z1t, hl, h1, yg, gg, d2, pair, mid, last, cnt, part, pr, hs, tot,
           w1v, w2v, labv, mskv,
           a_sem, in_sem, x_sent, x_got, y_sent, y_got, d_sent, d_got, c_sent, c_got, p_sent, p_got):
    r = lax.axis_index("rep")
    n = lax.axis_index("nodes")
    x, c = n // 2, n % 2

    def coords(rel):
        xx = 1 - x if rel & 4 else x
        yy = 1 - r if rel & 2 else r
        cc = 1 - c if rel & 1 else c
        return yy, 2 * xx + cc

    def peer(rel):
        yy, nn = coords(rel)
        return {"rep": yy, "nodes": nn}

    def send(src, dst, ssem, rsem, rel):
        pltpu.make_async_remote_copy(src_ref=src, dst_ref=dst, send_sem=ssem, recv_sem=rsem,
                                     device_id=peer(rel), device_id_type=MESH).start()

    def wait(ref, sem):
        pltpu.make_async_copy(ref, ref, sem).wait()

    ins = [pltpu.make_async_copy(feat, xg.at[0], in_sem.at[0]),
           pltpu.make_async_copy(w1, w1v, in_sem.at[1]),
           pltpu.make_async_copy(w2, w2v, in_sem.at[2]),
           pltpu.make_async_copy(lab, labv, in_sem.at[3]),
           pltpu.make_async_copy(msk, mskv, in_sem.at[4])]
    for cp in ins:
        cp.start()
    barrier = pltpu.get_barrier_semaphore()
    for s in (1, 2, 4):
        pl.semaphore_signal(barrier, inc=1, device_id=peer(s), device_id_type=MESH)
    loads = {}
    own_rows = pl.ds(pl.multiple_of(r * NB, NB), NB)
    for s in (0, 1, 4, 2, 5, 3, 6, 7):
        yy, nn = coords(s)
        columns = pl.ds(pl.multiple_of((2 * nn + yy) * NB, NB), NB)
        loads[s] = pltpu.make_async_copy(adj.at[own_rows, columns], a_own.at[s], a_sem.at[s])
        loads[s].start()
    ins[0].wait()
    pl.semaphore_wait(barrier, 3)

    def gather(view, sent, got, use, group, idle):
        half = PIECES // 2
        low, high = list(range(half)), list(range(half, PIECES))
        xseq, yseq = high + low, low + high

        def cp(src, dst, piece, rel, sem):
            send(view(src, piece, piece + 1), view(dst, piece, piece + 1), sent, got.at[sem], rel)

        def two(sem):
            wait(view(0, 0, 2), got.at[sem])

        for j in range(PIECES):
            cp(0, 4, xseq[j], 4, j)
            cp(0, 2, yseq[j], 2, j)
            if j == 0:
                send(view(0, 0, PIECES), view(1, 0, PIECES), sent, got.at[4 * PIECES - 1], 1)
        use([(0, i) for i in range(PIECES)])
        wait(view(1, 0, PIECES), got.at[4 * PIECES - 1])
        use([(1, i) for i in range(PIECES)])
        idle()
        ready, held = [], []

        def across(j):
            two(2 * PIECES + j)
            cp(6, 7, xseq[j], 1, 2 * PIECES + half + j)
            cp(6, 7, yseq[j], 1, 2 * PIECES + half + j)

        for j in range(PIECES):
            two(j)
            if j < half:
                cp(4, 6, xseq[j], 2, 2 * PIECES + j)
                cp(2, 6, yseq[j], 4, 2 * PIECES + j)
            cp(4, 5, xseq[j], 1, PIECES + j)
            cp(2, 3, yseq[j], 1, PIECES + j)
            ready += [(4, xseq[j]), (2, yseq[j])]
            if j % group == group - 1:
                for i in held:
                    two(PIECES + i)
                    ready += [(5, xseq[i]), (3, yseq[i])]
                held = []
                use(ready)
                ready = []
            held.append(j)
        held = held[-group:]
        across(0)
        for i in held:
            two(PIECES + i)
            ready += [(5, xseq[i]), (3, yseq[i])]
        use(ready)
        for j in range(1, half):
            across(j)
        use([(6, i) for i in range(PIECES)])
        for j in range(half):
            two(2 * PIECES + half + j)
        use([(7, i) for i in range(PIECES)])

    def xview(s, lo, hi):
        return xg.at[s, pl.ds(lo * XP, (hi - lo) * XP), :]

    started = {}

    def xuse(pieces):
        if not started:
            for cp in ins[1:]:
                cp.wait()
            started["b1"] = w1v[...].astype(BF16)
        parts = []
        for s, i in sorted(pieces):
            if s in loads:
                loads.pop(s).wait()
            if parts and parts[-1][0] == s and parts[-1][2] == i * XP:
                parts[-1][2] += XP
            else:
                parts.append([s, i * XP, i * XP + XP])
        for s, lo, hi in parts:
            rhs[s, lo:hi, HID:] = dot(xg[s, lo:hi, :], started["b1"]).astype(BF16)
            rhs[s, lo:hi, :HID] = xg[s, lo:hi, :]
        for m in range(0, NB, 256):
            prod = sum(dot(a_own[s, m:m + 256, lo:hi], rhs[s, lo:hi, :]) for s, lo, hi in parts)
            if "x" in started:
                acc[m:m + 256, :] += prod
            else:
                acc[m:m + 256, :] = prod
        started["x"] = True

    gather(xview, x_sent, x_got, xuse, 1, lambda: None)
    b2t = w2v[...].astype(BF16)
    b2 = w2v[...].T.astype(BF16)
    mask = mskv[...].astype(F32)
    cnt[0] = jnp.broadcast_to(jnp.sum(mask, axis=1, keepdims=True), (8, 128))

    z1 = acc[:, HID:]
    h1[...] = jnp.maximum(z1, 0.0).astype(BF16)
    y2 = dot(b2t, h1[...], 1, 1).astype(BF16)
    for i in range(PIECES):
        yg[0, i] = y2[:, i * XP:(i + 1) * XP]

    def yview(s, lo, hi):
        return yg.at[s, pl.ds(lo, hi - lo)]

    def yuse(pieces):
        parts = []
        for s, i in sorted(pieces):
            if parts and parts[-1][0] == s and parts[-1][2] == i:
                parts[-1][2] += 1
            else:
                parts.append([s, i, i + 1])
        for m in range(0, NB, HALF):
            prod = sum(dot(jnp.concatenate([yg[s, i] for i in range(lo, hi)], axis=1),
                           a_own[s, m:m + HALF, lo * XP:hi * XP], 1, 1) for s, lo, hi in parts)
            if "y" in started:
                z2t[:, m:m + HALF] += prod
            else:
                z2t[:, m:m + HALF] = prod
        started["y"] = True

    def keep_for_backward():
        for s in range(1, 8):
            send(cnt.at[0], cnt.at[s], c_sent, c_got, s)
        z1t[...] = acc[:, HID:].T
        ax = acc[:, :HID]
        high = ax.astype(BF16)
        hl[:, :HID] = high
        hl[:, HID:] = (ax - high.astype(F32)).astype(BF16)

    gather(yview, y_sent, y_got, yuse, 2, keep_for_backward)

    wait(cnt.at[pl.ds(1, 7)], c_got)
    total = cnt[0][0:1, 0:1]
    for s in range(1, 8):
        total = total + cnt[s][0:1, 0:1]
    z = z2t[...]
    z = z - jnp.max(z, axis=0, keepdims=True)
    logp = z - jnp.log(jnp.sum(jnp.exp(z), axis=0, keepdims=True))
    onehot = (labv[...] == lax.broadcasted_iota(jnp.int32, (CLS, NB), 0)).astype(F32)
    loss = -jnp.sum(mask * jnp.sum(onehot * logp, axis=0, keepdims=True), axis=1, keepdims=True)
    gg[...] = ((jnp.exp(logp) - onehot) * (mask / total)).astype(BF16)

    def partial(s, q0, q1):
        prod = dot(gg[...], a_own[s, :, q0 * XP:q1 * XP])
        for q in range(q0, q1):
            d2[s, q] = prod[:, (q - q0) * XP:(q - q0 + 1) * XP]

    def to_pair(s, q0, q1, sem):
        partial(s, q0, q1)
        send(d2.at[s, pl.ds(q0, q1 - q0)], pair.at[s // 2, pl.ds(q0, q1 - q0)], d_sent, d_got.at[sem], 1)

    def from_pair(s, q0, q1, sem):
        wait(pair.at[s // 2, pl.ds(q0, q1 - q0)], d_got.at[sem])
        d2[s, q0:q1] += pair[s // 2, q0:q1]

    to_pair(7, 0, 2, 0)
    to_pair(7, 2, 4, 1)
    partial(6, 0, 4)
    from_pair(6, 0, 2, 0)
    for j in range(2):
        send(d2.at[6, j], mid.at[j], d_sent, d_got.at[5 + j], 4)
    from_pair(6, 2, 4, 1)
    for j in range(2):
        send(d2.at[6, 2 + j], mid.at[2 + j], d_sent, d_got.at[5 + j], 2)
    to_pair(5, 0, 4, 2)
    to_pair(3, 0, 4, 3)
    partial(4, 0, 4)
    from_pair(4, 0, 4, 2)
    send(d2.at[4, pl.ds(0, 2)], last.at[0, pl.ds(0, 2)], d_sent, d_got.at[7], 4)
    partial(2, 0, 4)
    from_pair(2, 0, 4, 3)
    send(d2.at[2, pl.ds(2, 2)], last.at[0, pl.ds(2, 2)], d_sent, d_got.at[7], 2)
    to_pair(1, 0, 4, 4)
    partial(0, 0, 4)
    from_pair(0, 0, 4, 4)
    for j in range(2):
        wait(mid.at[pl.ds(0, 2)], d_got.at[5 + j])
        d2[2, j] += mid[j]
        send(d2.at[2, j], last.at[1, j], d_sent, d_got.at[8 + j], 2)
        d2[4, 2 + j] += mid[2 + j]
        send(d2.at[4, 2 + j], last.at[1, 2 + j], d_sent, d_got.at[8 + j], 4)
    wait(last.at[0], d_got.at[7])
    d2[0] += last[0]
    for j in range(2):
        wait(mid.at[pl.ds(0, 2)], d_got.at[8 + j])
    d2b = jnp.concatenate([(d2[0, q] + last[1, q]).astype(BF16) for q in range(PIECES)], axis=1)

    g1 = jnp.where(z1t[...] > 0, dot(b2, d2b), 0.0).astype(BF16)
    dw1 = dot(g1, hl[...])
    part[0:HID] = dw1[:, :HID] + dw1[:, HID:]
    part[HID:HID + CLS] = dot(d2b, h1[...])
    part[HID + CLS:] = jnp.broadcast_to(loss, (8, 128))

    mine = pl.ds(pl.multiple_of(c * PHALF, 8), PHALF)
    theirs = pl.ds(pl.multiple_of((1 - c) * PHALF, 8), PHALF)
    send(part.at[theirs, :], pr, p_sent, p_got.at[0], 1)
    wait(pr, p_got.at[0])
    hs[0] = part[mine, :] + pr[...]
    for k, rel in ((3, 6), (1, 4), (2, 2)):
        send(hs.at[0], hs.at[k], p_sent, p_got.at[1], rel)
    wait(hs.at[pl.ds(1, 3)], p_got.at[1])
    tot[mine, :] = (hs[0] + hs[1]) + (hs[2] + hs[3])
    send(tot.at[mine, :], tot.at[mine, :], p_sent, p_got.at[2], 1)
    wait(pr, p_got.at[2])
    out[0:HID + CLS, :] = tot[0:HID + CLS, :]
    out[HID + CLS:, :] = tot[HID + CLS:, :] / total

    wait(xg.at[pl.ds(0, 7)], x_sent)
    wait(yg.at[pl.ds(0, 7)], y_sent)
    wait(cnt.at[pl.ds(0, 7)], c_sent)
    wait(d2.at[pl.ds(0, 7)], d_sent)
    wait(hs, p_sent)


def unpack(packed, o_loss, o_dw1, o_dw2):
    o_dw1[...] = packed[0:HID].T
    o_dw2[...] = packed[HID:HID + CLS]
    o_loss[...] = packed[HID + CLS:HID + CLS + 1, 0:1]


def solution(mesh):
    any_spec = pl.BlockSpec(memory_space=pl.ANY)
    vmem_spec = pl.BlockSpec(memory_space=pltpu.VMEM)
    dma = pltpu.SemaphoreType.DMA

    call = pl.pallas_call(
        kernel,
        out_shape=jax.ShapeDtypeStruct((PART, 128), F32),
        in_specs=[any_spec] * 6,
        out_specs=vmem_spec,
        scratch_shapes=[
            pltpu.VMEM((8, NB, NB), BF16),
            pltpu.VMEM((8, NB, HID), BF16),
            pltpu.VMEM((8, NB, 2 * HID), BF16),
            pltpu.VMEM((NB, 2 * HID), F32),
            pltpu.VMEM((CLS, NB), F32),
            pltpu.VMEM((HID, NB), F32),
            pltpu.VMEM((NB, 2 * HID), BF16),
            pltpu.VMEM((NB, HID), BF16),
            pltpu.VMEM((8, PIECES, CLS, XP), BF16),
            pltpu.VMEM((CLS, NB), BF16),
            pltpu.VMEM((8, PIECES, CLS, XP), F32),
            pltpu.VMEM((4, PIECES, CLS, XP), F32),
            pltpu.VMEM((PIECES, CLS, XP), F32),
            pltpu.VMEM((2, PIECES, CLS, XP), F32),
            pltpu.VMEM((8, 8, 128), F32),
            pltpu.VMEM((PART, 128), F32),
            pltpu.VMEM((PHALF, 128), F32),
            pltpu.VMEM((5, PHALF, 128), F32),
            pltpu.VMEM((PART, 128), F32),
            pltpu.VMEM((HID, HID), F32),
            pltpu.VMEM((CLS, HID), F32),
            pltpu.VMEM((1, NB), jnp.int32),
            pltpu.VMEM((1, NB), jnp.int32),
            dma((8,)), dma((5,)), dma, dma((4 * PIECES,)), dma, dma((4 * PIECES,)), dma, dma((10,)),
            dma, dma, dma, dma((3,)),
        ],
        compiler_params=pltpu.CompilerParams(collective_id=0, has_side_effects=True,
                                             vmem_limit_bytes=40 << 20),
        name="gcn_step",
    )

    unpack_call = pl.pallas_call(
        unpack,
        out_shape=(jax.ShapeDtypeStruct((1, 1), F32), jax.ShapeDtypeStruct((HID, HID), F32),
                   jax.ShapeDtypeStruct((CLS, HID), F32)),
        in_specs=[vmem_spec],
        out_specs=(vmem_spec,) * 3,
        compiler_params=pltpu.CompilerParams(vmem_limit_bytes=4 << 20),
        name="unpack",
    )

    def local_step(adj_rows, features, w_one, w_two, labels, label_mask):
        operands = (adj_rows, features, w_one, w_two.T, labels.reshape(1, NB), label_mask.reshape(1, NB))
        packed = call(*(pltpu.with_memory_space_constraint(v, pltpu.HBM) for v in operands))
        loss, dw1, dw2 = unpack_call(packed)
        return loss.reshape(()), dw1, dw2.T

    row_spec = P(("nodes", "rep"))
    return jax.shard_map(local_step, mesh=mesh,
                         in_specs=(P("nodes", None), P(("nodes", "rep"), None), P(), P(), row_spec, row_spec),
                         out_specs=(P(), P(), P()), check_vma=False)
```

time: 44.3 us -> 42.6 us (0.962)
  Pallas kernels: 43.6 us -> 41.8 us
    pallas_call x1, Pallas kernels: 42.9 us -> 41.1 us  [local_step(): call(*(pltpu.with_memory_space_constraint(v, pltpu.HBM) for v in operands))]
where the time goes in v4:
time: 42.6 us; the launch traced here: 42.5 us
  Pallas kernels  41.8 us (98%)
  between operations  0.64 us (2%)
    pallas_call x1, Pallas kernels, local_step(): call(*(pltpu.with_memory_space_constraint(v, pltpu.HBM) for v in operands))  41.1 us

profile of v4, /device:TPU:0, one launch (start us, length us, event | category | flops | bytes accessed | tf_op | source)
XLA Modules:
  0.0 42.5 jit_solution(4986861492531619400)
XLA Ops:
  0.6 41.1 %gcn_step.1.packed = f32[176,128]{1,0:T(8,128)S(1)} custom-call(bf16[2048,8192]{1,0:T(8,128)(2,1)} %adj.1, bf16[1024,128]{1,0:T(8,128)(2,1)} %feat.1, f32[128,128]{1,0:T(8,128)} %w1.1, f32[40,128]{1,0:T(8,128)} %bitcast.5, s32[1,1024]{1,0:T(1,128)} %bitcast.6, s32[1,1024]{1,0:T(1,128)} %bitcast.7), custom_call_target="tpu_custom_call" | custom-call | tf_op jit(solution)/shard_map/gcn_step/pallas_call | solution.py:339
  41.8 0.7 %unpack.1 = (f32[1,1]{1,0:T(1,128)}, f32[128,128]{1,0:T(8,128)}, f32[40,128]{1,0:T(8,128)}) custom-call(f32[176,128]{1,0:T(8,128)S(1)} %gcn_step.1.packed), custom_call_target="tpu_custom_call" | custom-call | tf_op jit(solution)/shard_map/unpack/pallas_call | solution.py:340

commit v5 on v4

--- a/solution.py
+++ b/solution.py
@@ -105,11 +105,8 @@
                 for i in held:
                     two(PIECES + i)
                     ready += [(5, xseq[i]), (3, yseq[i])]
-                held = []
                 use(ready)
-                ready = []
-            held.append(j)
-        held = held[-group:]
+                ready, held = [], list(range(j - group + 1, j + 1))
         across(0)
         for i in held:
             two(PIECES + i)
@@ -217,36 +214,47 @@
         wait(pair.at[s // 2, pl.ds(q0, q1 - q0)], d_got.at[sem])
         d2[s, q0:q1] += pair[s // 2, q0:q1]
 
-    to_pair(7, 0, 2, 0)
-    to_pair(7, 2, 4, 1)
+    def stage_one(q):
+        from_pair(6, q, q + 1, q)
+        send(d2.at[6, q], mid.at[q], d_sent, d_got.at[9 + q % 2], 4 if q < 2 else 2)
+
+    to_pair(7, 0, 1, 0)
+    to_pair(7, 2, 3, 2)
     partial(6, 0, 4)
-    from_pair(6, 0, 2, 0)
+    to_pair(7, 1, 2, 1)
+    stage_one(0)
+    to_pair(7, 3, 4, 3)
+    stage_one(2)
+    to_pair(5, 0, 2, 4)
+    stage_one(1)
+    to_pair(3, 2, 4, 5)
+    stage_one(3)
+    partial(4, 0, 2)
+    partial(2, 2, 4)
+    from_pair(4, 0, 2, 4)
+    send(d2.at[4, pl.ds(0, 2)], last.at[0, pl.ds(0, 2)], d_sent, d_got.at[11], 4)
+    from_pair(2, 2, 4, 5)
+    send(d2.at[2, pl.ds(2, 2)], last.at[0, pl.ds(2, 2)], d_sent, d_got.at[11], 2)
+    to_pair(5, 2, 4, 6)
+    to_pair(3, 0, 2, 7)
+    partial(4, 2, 4)
+    partial(2, 0, 2)
+    to_pair(1, 0, 4, 8)
+    from_pair(4, 2, 4, 6)
+    from_pair(2, 0, 2, 7)
     for j in range(2):
-        send(d2.at[6, j], mid.at[j], d_sent, d_got.at[5 + j], 4)
-    from_pair(6, 2, 4, 1)
-    for j in range(2):
-        send(d2.at[6, 2 + j], mid.at[2 + j], d_sent, d_got.at[5 + j], 2)
-    to_pair(5, 0, 4, 2)
-    to_pair(3, 0, 4, 3)
-    partial(4, 0, 4)
-    from_pair(4, 0, 4, 2)
-    send(d2.at[4, pl.ds(0, 2)], last.at[0, pl.ds(0, 2)], d_sent, d_got.at[7], 4)
-    partial(2, 0, 4)
-    from_pair(2, 0, 4, 3)
-    send(d2.at[2, pl.ds(2, 2)], last.at[0, pl.ds(2, 2)], d_sent, d_got.at[7], 2)
-    to_pair(1, 0, 4, 4)
-    partial(0, 0, 4)
-    from_pair(0, 0, 4, 4)
-    for j in range(2):
-        wait(mid.at[pl.ds(0, 2)], d_got.at[5 + j])
+        wait(mid.at[pl.ds(0, 2)], d_got.at[9 + j])
         d2[2, j] += mid[j]
-        send(d2.at[2, j], last.at[1, j], d_sent, d_got.at[8 + j], 2)
+        send(d2.at[2, j], last.at[1, j], d_sent, d_got.at[12 + j], 2)
         d2[4, 2 + j] += mid[2 + j]
-        send(d2.at[4, 2 + j], last.at[1, 2 + j], d_sent, d_got.at[8 + j], 4)
-    wait(last.at[0], d_got.at[7])
+        send(d2.at[4, 2 + j], last.at[1, 2 + j], d_sent, d_got.at[12 + j], 4)
+        if j == 0:
+            partial(0, 0, 4)
+    from_pair(0, 0, 4, 8)
+    wait(last.at[0], d_got.at[11])
     d2[0] += last[0]
     for j in range(2):
-        wait(mid.at[pl.ds(0, 2)], d_got.at[8 + j])
+        wait(mid.at[pl.ds(0, 2)], d_got.at[12 + j])
     d2b = jnp.concatenate([(d2[0, q] + last[1, q]).astype(BF16) for q in range(PIECES)], axis=1)
 
     g1 = jnp.where(z1t[...] > 0, dot(b2, d2b), 0.0).astype(BF16)
@@ -316,7 +324,7 @@
             pltpu.VMEM((CLS, HID), F32),
             pltpu.VMEM((1, NB), jnp.int32),
             pltpu.VMEM((1, NB), jnp.int32),
-            dma((8,)), dma((5,)), dma, dma((4 * PIECES,)), dma, dma((4 * PIECES,)), dma, dma((10,)),
+            dma((8,)), dma((5,)), dma, dma((4 * PIECES,)), dma, dma((4 * PIECES,)), dma, dma((14,)),
             dma, dma, dma, dma((3,)),
         ],
         compiler_params=pltpu.CompilerParams(collective_id=0, has_side_effects=True,

time: 42.6 us -> 41.3 us (0.969)
  Pallas kernels: 41.8 us -> 40.6 us
    pallas_call x1, Pallas kernels: 41.1 us -> 39.8 us  [local_step(): call(*(pltpu.with_memory_space_constraint(v, pltpu.HBM) for v in operands))]
where the time goes in v5:
time: 41.3 us; the launch traced here: 41.2 us
  Pallas kernels  40.6 us (98%)
  between operations  0.64 us (2%)
    pallas_call x1, Pallas kernels, local_step(): call(*(pltpu.with_memory_space_constraint(v, pltpu.HBM) for v in operands))  39.8 us

profile of v5, /device:TPU:0, one launch (start us, length us, event | category | flops | bytes accessed | tf_op | source)
XLA Modules:
  0.0 41.2 jit_solution(11935055268106047504)
XLA Ops:
  0.6 39.8 %gcn_step.1.packed = f32[176,128]{1,0:T(8,128)S(1)} custom-call(bf16[2048,8192]{1,0:T(8,128)(2,1)} %adj.1, bf16[1024,128]{1,0:T(8,128)(2,1)} %feat.1, f32[128,128]{1,0:T(8,128)} %w1.1, f32[40,128]{1,0:T(8,128)} %bitcast.5, s32[1,1024]{1,0:T(1,128)} %bitcast.6, s32[1,1024]{1,0:T(1,128)} %bitcast.7), custom_call_target="tpu_custom_call" | custom-call | tf_op jit(solution)/shard_map/gcn_step/pallas_call | solution.py:347
  40.5 0.7 %unpack.1 = (f32[1,1]{1,0:T(1,128)}, f32[128,128]{1,0:T(8,128)}, f32[40,128]{1,0:T(8,128)}) custom-call(f32[176,128]{1,0:T(8,128)S(1)} %gcn_step.1.packed), custom_call_target="tpu_custom_call" | custom-call | tf_op jit(solution)/shard_map/unpack/pallas_call | solution.py:348
